TPU v7x, 32 devices: a whole 2x2x4 slice. The times are simulated.
32 devices in a mesh: gx: 4 (over x, core), gy: 8 (over z, y).
Axes of the slice: x: 2, y: 2, z: 4, core: 2. Of those that a mesh axis runs over, the one named last changes fastest.
Arguments:
- right_side: float32 [2, 64, 256, 128], P(None, 'gx', 'gy'), may hold values from -6 to 6
- wavenumber: float32 [64, 256, 128], P('gx', 'gy'), may hold values from 0.2 to 1
- pml_layer: int32 [64, 256, 128], P('gx', 'gy'), may hold values from 0 to 3
- aggregate: int32 [64, 256, 128], P('gx', 'gy'), may hold values from 0 to 15, as said below
- coarse_inverse: float32 [2, 512, 512], P(None, ('gx', 'gy')), may hold values from -0.0029296875 to 0.0029296875
Outputs:
- solution: float32 [2, 64, 256, 128], P(None, 'gx', 'gy')
- hessenberg: float32 [2, 5, 4], replicated
Inputs may be any that keep to these rules, and one draw needn't show every extreme that they name: `aggregate`: along the third dimension the value never falls, and every value of 0 to 15 occurs in every column of cells.
All inputs are finite; a program needn't handle non-finite values.
Results may differ from a plain program's by a relative error of at most 0.00015.
Values sent between devices are 32-bit elements; how exact they have to be, the bound alone decides.
No kernel may reach another device: no remote copies, remote signals or barrier semaphores. Data moves between devices by JAX's collectives and lax.ppermute only.
A program may use at most 64 MiB of HBM per device.

v0:
```python
import math
import jax
import jax.numpy as jnp
from jax import lax
from jax.sharding import PartitionSpec as P

ITERS = 4
damping = 0.8
pml_strength = 3.0
epsilon = 1e-06


def with_halo(block, sides, width):
    for axis, dim in sides:
        count = lax.axis_size(axis)
        forward = [(i, i + 1) for i in range(count - 1)]
        backward = [(target, source) for source, target in forward]
        low = lax.ppermute(
            lax.slice_in_dim(block, block.shape[dim] - width, None, axis=dim), axis, forward
        )
        high = lax.ppermute(lax.slice_in_dim(block, 0, width, axis=dim), axis, backward)
        block = jnp.concatenate([low, block, high], axis=dim)
    return block


def coefficients(wavenumber, layer_float):
    wave_sq = wavenumber * wavenumber
    depth = layer_float / 3.0
    absorb = wave_sq * (pml_strength * depth * depth)
    diag_re = 6.0 - wave_sq
    magnitude = diag_re * diag_re + absorb * absorb
    return (wave_sq, absorb, damping * diag_re / magnitude, damping * absorb / magnitude)


def operate_inner(extended, wave_sq, absorb):
    middle = extended[:, 1:-1, 1:-1]
    above = jnp.concatenate([middle[..., 1:], jnp.zeros_like(middle[..., :1])], -1)
    below = jnp.concatenate([jnp.zeros_like(middle[..., :1]), middle[..., :-1]], -1)
    beside = (
        extended[:, 2:, 1:-1]
        + extended[:, :-2, 1:-1]
        + extended[:, 1:-1, 2:]
        + extended[:, 1:-1, :-2]
        + above
        + below
    )
    real_part = (6.0 - wave_sq) * middle[0] - beside[0] + absorb * middle[1]
    imag_part = (6.0 - wave_sq) * middle[1] - beside[1] - absorb * middle[0]
    return jnp.stack([real_part, imag_part])


def smooth(field, scale_re, scale_im):
    return jnp.stack(
        [scale_re * field[0] - scale_im * field[1], scale_re * field[1] + scale_im * field[0]]
    )


def complex_scale(scale_re, scale_im, field):
    return jnp.stack(
        [scale_re * field[0] - scale_im * field[1], scale_re * field[1] + scale_im * field[0]]
    )


def inner_local(left, right):
    return jnp.stack(
        [
            jnp.sum(left[0] * right[0] + left[1] * right[1]),
            jnp.sum(left[0] * right[1] - left[1] * right[0]),
        ]
    )


def least_squares(hessenberg, beta):
    real_h = hessenberg[0]
    imag_h = hessenberg[1]
    stacked = jnp.concatenate(
        [jnp.concatenate([real_h, -imag_h], 1), jnp.concatenate([imag_h, real_h], 1)], 0
    )
    count = stacked.shape[1]
    target = jnp.zeros((stacked.shape[0],), jnp.float32).at[0].set(beta)
    ortho = []
    upper = {}
    for column in range(count):
        vector = stacked[:, column]
        for position in range(column):
            upper[position, column] = jnp.zeros((), jnp.float32)
        for repeat in range(2):
            for position in range(len(ortho)):
                weight = jnp.sum(ortho[position] * vector)
                vector = vector - weight * ortho[position]
                upper[position, column] = upper[position, column] + weight
        norm_value = jnp.sqrt(jnp.sum(vector * vector))
        upper[column, column] = norm_value
        ortho.append(vector / norm_value)
    project = [jnp.sum(basis_vec * target) for basis_vec in ortho]
    solved = [None] * count
    for column in reversed(range(count)):
        total = project[column]
        for later in range(column + 1, count):
            total = total - upper[column, later] * solved[later]
        solved[column] = total / upper[column, column]
    return solved


def restrict(flat_field, flat_ids, levels_count):
    total = flat_ids.shape[0]
    block = math.gcd(total, 16384)
    levels = jnp.arange(levels_count, dtype=jnp.int32)

    def accumulate(step_index, result):
        piece = lax.dynamic_slice_in_dim(flat_field, step_index * block, block, 1)
        labels = lax.dynamic_slice_in_dim(flat_ids, step_index * block, block, 0)
        onehot = (labels[None, :] == levels[:, None]).astype(jnp.float32)
        return result + lax.dot_general(
            piece, onehot, (((1,), (1,)), ((), ())), precision=lax.Precision.HIGHEST
        )

    return lax.fori_loop(0, total // block, accumulate, jnp.zeros((2, levels_count), jnp.float32))


def prolong(values, flat_ids):
    total = flat_ids.shape[0]
    block = math.gcd(total, 16384)
    levels = jnp.arange(values.shape[1], dtype=jnp.int32)

    def place(step_index, result):
        labels = lax.dynamic_slice_in_dim(flat_ids, step_index * block, block, 0)
        onehot = (levels[:, None] == labels[None, :]).astype(jnp.float32)
        piece = jnp.dot(values, onehot, precision=lax.Precision.HIGHEST)
        return lax.dynamic_update_slice_in_dim(result, piece, step_index * block, 1)

    return lax.fori_loop(0, total // block, place, jnp.zeros((2, total), jnp.float32))


def coarse_fix(remainder, flat_ids, coarse_inverse):
    highest = lax.Precision.HIGHEST
    levels_count = coarse_inverse.shape[1]
    total_coarse = coarse_inverse.shape[2]
    partial_value = restrict(remainder.reshape(2, -1), flat_ids, levels_count)
    offset = (lax.axis_index("gx") * lax.axis_size("gy") + lax.axis_index("gy")) * levels_count
    padded = lax.dynamic_update_slice(
        jnp.zeros((2, total_coarse), jnp.float32), partial_value, (jnp.zeros((), jnp.int32), offset)
    )
    whole = lax.psum(padded, ("gx", "gy"))
    own_re = jnp.dot(coarse_inverse[0], whole[0], precision=highest) - jnp.dot(
        coarse_inverse[1], whole[1], precision=highest
    )
    own_im = jnp.dot(coarse_inverse[0], whole[1], precision=highest) + jnp.dot(
        coarse_inverse[1], whole[0], precision=highest
    )
    return prolong(jnp.stack([own_re, own_im]), flat_ids).reshape(remainder.shape)


def operate_near(field, wave_sq, absorb):
    extended = with_halo(field, (("gx", 1), ("gy", 2)), 1)
    return operate_inner(extended, wave_sq, absorb)


def operate_final(field, wave_sq, absorb):
    extended = with_halo(field, (("gx", 1), ("gy", 2)), 1)
    return operate_inner(extended, wave_sq, absorb)


def body(right_side, wavenumber, pml_layer, aggregate, coarse_inverse):
    layer_float = pml_layer.astype(jnp.float32)
    wave_sq, absorb, scale_re, scale_im = coefficients(wavenumber, layer_float)
    flat_ids = aggregate.reshape(-1)
    beta = jnp.sqrt(lax.psum(jnp.sum(right_side * right_side), ("gx", "gy")) + epsilon)
    basis = [right_side / beta]
    directions = []
    columns_re = []
    columns_im = []
    for column in range(ITERS):
        vector = basis[column]
        first = smooth(vector, scale_re, scale_im)
        second = first + smooth(vector - operate_near(first, wave_sq, absorb), scale_re, scale_im)
        remainder = vector - operate_near(second, wave_sq, absorb)
        direction = second + coarse_fix(remainder, flat_ids, coarse_inverse)
        image = operate_final(direction, wave_sq, absorb)
        local_dots = jnp.stack([inner_local(member, image) for member in basis], 1)
        dots, squared = lax.psum((local_dots, jnp.sum(image * image)), ("gx", "gy"))
        for position in range(len(basis)):
            image = image - complex_scale(dots[0, position], dots[1, position], basis[position])
        leftover = squared - jnp.sum(dots * dots)
        length = jnp.sqrt(jnp.maximum(leftover, 0.0) + epsilon)
        tail = jnp.zeros((ITERS - 1 - column,), jnp.float32)
        columns_re.append(jnp.concatenate([dots[0], length[None], tail]))
        columns_im.append(jnp.concatenate([dots[1], jnp.zeros((1,), jnp.float32), tail]))
        directions.append(direction)
        if column + 1 < ITERS:
            basis.append(image / length)
    hessenberg = jnp.stack([jnp.stack(columns_re, 1), jnp.stack(columns_im, 1)])
    solved = least_squares(hessenberg, beta)
    solution = jnp.zeros_like(right_side)
    for column in range(ITERS):
        solution = solution + complex_scale(
            solved[column], solved[ITERS + column], directions[column]
        )
    return (solution, hessenberg)


def solution(mesh):
    return jax.shard_map(
        body,
        mesh=mesh,
        in_specs=(
            P(None, "gx", "gy", None),
            P("gx", "gy", None),
            P("gx", "gy", None),
            P("gx", "gy", None),
            P(None, ("gx", "gy"), None),
        ),
        out_specs=(P(None, "gx", "gy", None), P()),
        check_vma=False,
    )
```

profile of v0, /device:TPU:0, one launch (start us, length us, event | category | flops | bytes accessed | tf_op | source)
XLA Modules:
  0.0 809.6 jit_solution(285482413600228902)
XLA Ops:
  2.5 42.2 %psum.91 = f32[]{:T(128)} all-reduce(f32[]{:T(128)} %multiply_reduce_fusion.3), channel_id=1, replica_groups=mesh['gx'=4,'gy'=8] {'gx','gy'}, use_global_device_ids=true, to_apply=%region_1.0 | all-reduce | flops 1 | bytes 8 | tf_op jit(solution)/shard_map/psum | solution.py:168
  53.2 5.0 collective-permute-start.3
  67.5 5.4 collective-permute-start.7
  76.2 7.0 while.117
  83.3 46.5 %psum.92 = f32[2,512]{1,0:T(2,128)S(1)} all-reduce(f32[2,512]{1,0:T(2,128)S(1)} %dynamic_update_slice.40), channel_id=1, replica_groups=mesh['gx'=4,'gy'=8] {'gx','gy'}, use_global_device_ids=true, to_apply=%region_4.0 | all-reduce | flops 1024 | bytes 8192 | tf_op jit(solution)/shard_map/psum | solution.py:144
  149.7 43.8 %all-reduce.29 = (f32[2,1]{0,1:T(1,128)S(1)}, f32[]{:T(128)}) all-reduce(f32[2,1]{0,1:T(1,128)S(1)} %maximum_bitcast_fusion.1, f32[]{:T(128)} %multiply_reduce_fusion.2), channel_id=1, replica_groups=mesh['gx'=4,'gy'=8] {'gx','gy'}, use_global_device_ids=true, to_apply=%region_9.0 | all-reduce | flops 3 | bytes 24 | tf_op jit(solution)/shard_map/psum | solution.py:181
  204.4 5.0 collective-permute-start.15
  220.2 5.6 collective-permute-start.19
  230.3 6.9 while.118
  237.5 47.6 %psum.95 = f32[2,512]{1,0:T(2,128)S(1)} all-reduce(f32[2,512]{1,0:T(2,128)S(1)} %dynamic_update_slice.41), channel_id=1, replica_groups=mesh['gx'=4,'gy'=8] {'gx','gy'}, use_global_device_ids=true, to_apply=%region_15.0 | all-reduce | flops 1024 | bytes 8192 | tf_op jit(solution)/shard_map/psum | solution.py:144
  295.7 4.8 collective-permute-start.23
  306.9 43.6 %all-reduce.28 = (f32[2,2]{0,1:T(2,128)S(1)}, f32[]{:T(128)}) all-reduce(f32[2,2]{0,1:T(2,128)S(1)} %pad_maximum_fusion.166, f32[]{:T(128)} %multiply_reduce_fusion.1), channel_id=1, replica_groups=mesh['gx'=4,'gy'=8] {'gx','gy'}, use_global_device_ids=true, to_apply=%region_22.0 | all-reduce | flops 5 | bytes 40 | tf_op jit(solution)/shard_map/psum | solution.py:181
  362.6 5.0 collective-permute-start.27
  377.5 5.3 collective-permute-start.31
  388.2 6.9 while.119
  395.3 47.6 %psum.98 = f32[2,512]{1,0:T(2,128)S(1)} all-reduce(f32[2,512]{1,0:T(2,128)S(1)} %dynamic_update_slice.42), channel_id=1, replica_groups=mesh['gx'=4,'gy'=8] {'gx','gy'}, use_global_device_ids=true, to_apply=%region_28.0 | all-reduce | flops 1024 | bytes 8192 | tf_op jit(solution)/shard_map/psum | solution.py:144
  453.6 4.8 collective-permute-start.35
  467.3 43.7 %all-reduce.27 = (f32[2,3]{0,1:T(4,128)S(1)}, f32[]{:T(128)}) all-reduce(f32[2,3]{0,1:T(4,128)S(1)} %pad_maximum_fusion.161, f32[]{:T(128)} %multiply_reduce_fusion), channel_id=1, replica_groups=mesh['gx'=4,'gy'=8] {'gx','gy'}, use_global_device_ids=true, to_apply=%region_37.0 | all-reduce | flops 7 | bytes 56 | tf_op jit(solution)/shard_map/psum | solution.py:181
  528.0 5.1 collective-permute-start.39
  542.8 5.5 collective-permute-start.43
  552.9 6.9 while.120
  560.0 47.0 %psum.101 = f32[2,512]{1,0:T(2,128)S(1)} all-reduce(f32[2,512]{1,0:T(2,128)S(1)} %dynamic_update_slice.43), channel_id=1, replica_groups=mesh['gx'=4,'gy'=8] {'gx','gy'}, use_global_device_ids=true, to_apply=%region_43.0 | all-reduce | flops 1024 | bytes 8192 | tf_op jit(solution)/shard_map/psum | solution.py:144
  620.8 4.8 collective-permute-start.47
  636.3 43.7 %all-reduce.26 = (f32[2,4]{0,1:T(4,128)S(1)}, f32[]{:T(128)}) all-reduce(f32[2,4]{0,1:T(4,128)S(1)} %pad_maximum_fusion.162, f32[]{:T(128)} %fusion.133), channel_id=1, replica_groups=mesh['gx'=4,'gy'=8] {'gx','gy'}, use_global_device_ids=true, to_apply=%region_54.0 | all-reduce | flops 9 | bytes 72 | tf_op jit(solution)/shard_map/psum | solution.py:181
  (514 shorter events, 302.2 us)
Async XLA Ops:
  51.9 6.5 collective-permute-start.2
  53.2 6.5 collective-permute-start.3
  66.2 7.0 collective-permute-start.6
  67.5 6.9 collective-permute-start.7
  138.9 6.3 collective-permute-start.10
  140.2 6.3 collective-permute-start.11
  203.1 6.5 collective-permute-start.14
  204.4 6.4 collective-permute-start.15
  218.9 7.1 collective-permute-start.18
  220.2 6.6 collective-permute-start.19
  294.4 6.3 collective-permute-start.22
  295.7 6.3 collective-permute-start.23
  361.3 6.5 collective-permute-start.26
  362.6 6.4 collective-permute-start.27
  376.2 6.9 collective-permute-start.30
  377.5 6.6 collective-permute-start.31
  452.3 6.3 collective-permute-start.34
  453.6 6.3 collective-permute-start.35
  526.7 6.6 collective-permute-start.38
  528.0 6.5 collective-permute-start.39
  541.5 7.1 collective-permute-start.42
  542.8 6.8 collective-permute-start.43
  619.5 6.3 collective-permute-start.46
  620.8 6.3 collective-permute-start.47
  (92 other events, 1041.4 us)
where the time goes:
time: 821 us; the launch traced here: 810 us
  blocking collectives  406 us (49%)
  other arithmetic  135 us (16%)
  starting transfers between devices  129 us (16%)
  between operations  54.6 us (7%)
  matrix products  39.1 us (5%)
  waiting for transfers between devices  23 us (3%)
  local copies, waits for them, and re-layouts  22.3 us (3%)
    psum x4, blocking collectives, coarse_fix(): whole = lax.psum(padded, ('gx', 'gy'))  189 us
    psum x4, blocking collectives, body(): dots, squared = lax.psum((local_dots, jnp.sum(image * image)), ('gx', 'gy'))  175 us
    ppermute x24, starting transfers between devices, with_halo(): lax.ppermute(lax.slice_in_dim(block, block.shape[dim] - width, None, axis...  98.4 us
    reduce_sum x34, other arithmetic, least_squares(): weight = jnp.sum(ortho[position] * vector)  64.5 us
    psum x1, blocking collectives, body(): lax.psum(jnp.sum(right_side * right_side), ('gx', 'gy')) + epsilon  42.2 us
    ppermute x24, starting transfers between devices, with_halo(): lax.ppermute(lax.slice_in_dim(block, 0, width, axis=dim), axis, backward)  31 us
    dot_general x16, matrix products, accumulate(): lax.dot_general(piece, onehot, (((1,), (1,)), ((), ())), precision=lax.Pr...  27.2 us
    ppermute x24, waiting for transfers between devices, with_halo(): lax.ppermute(lax.slice_in_dim(block, block.shape[dim] - width, None, axis...  22.9 us
  transfers between devices with their start and end apart: 48, of which 23 were waited for; matrix products, arithmetic and copies ran while one was open for 1% of the time, Pallas kernels for 0%

commit v1 on v0

--- a/solution.py
+++ b/solution.py
@@ -141,7 +141,7 @@
     padded = lax.dynamic_update_slice(
         jnp.zeros((2, total_coarse), jnp.float32), partial_value, (jnp.zeros((), jnp.int32), offset)
     )
-    whole = lax.psum(padded, ("gx", "gy"))
+    whole = lax.psum(lax.psum(padded, "gy"), "gx")
     own_re = jnp.dot(coarse_inverse[0], whole[0], precision=highest) - jnp.dot(
         coarse_inverse[1], whole[1], precision=highest
     )

time: 821 us -> 754 us (0.918)
  blocking collectives: 406 us -> 340 us
    psum x4 -> x8, blocking collectives: 189 us -> 130 us  [coarse_fix(): whole = lax.psum(lax.psum(padded, 'gy'), 'gx')]
where the time goes in v1:
time: 754 us; the launch traced here: 743 us
  blocking collectives  340 us (45%)
  other arithmetic  135 us (18%)
  starting transfers between devices  128 us (17%)
  between operations  54.6 us (7%)
  matrix products  39.1 us (5%)
  waiting for transfers between devices  23.3 us (3%)
  local copies, waits for them, and re-layouts  22.3 us (3%)
    psum x4, blocking collectives, body(): dots, squared = lax.psum((local_dots, jnp.sum(image * image)), ('gx', 'gy'))  168 us
    psum x8, blocking collectives, coarse_fix(): whole = lax.psum(lax.psum(padded, 'gy'), 'gx')  130 us
    ppermute x24, starting transfers between devices, with_halo(): lax.ppermute(lax.slice_in_dim(block, block.shape[dim] - width, None, axis...  97.2 us
    reduce_sum x34, other arithmetic, least_squares(): weight = jnp.sum(ortho[position] * vector)  64.5 us
    psum x1, blocking collectives, body(): lax.psum(jnp.sum(right_side * right_side), ('gx', 'gy')) + epsilon  42.2 us
    ppermute x24, starting transfers between devices, with_halo(): lax.ppermute(lax.slice_in_dim(block, 0, width, axis=dim), axis, backward)  31 us
    dot_general x16, matrix products, accumulate(): lax.dot_general(piece, onehot, (((1,), (1,)), ((), ())), precision=lax.Pr...  27.2 us
    ppermute x24, waiting for transfers between devices, with_halo(): lax.ppermute(lax.slice_in_dim(block, block.shape[dim] - width, None, axis...  23.3 us
  transfers between devices with their start and end apart: 48, of which 23 were waited for; matrix products, arithmetic and copies ran while one was open for 1% of the time, Pallas kernels for 0%

profile of v1, /device:TPU:0, one launch (start us, length us, event | category | flops | bytes accessed | tf_op | source)
XLA Modules:
  0.0 742.7 jit_solution(1943604673079011715)
XLA Ops:
  2.5 42.2 %psum.119 = f32[]{:T(128)} all-reduce(f32[]{:T(128)} %multiply_reduce_fusion.3), channel_id=1, replica_groups=mesh['gx'=4,'gy'=8] {'gx','gy'}, use_global_device_ids=true, to_apply=%region_1.0 | all-reduce | flops 1 | bytes 8 | tf_op jit(solution)/shard_map/psum | solution.py:168
  53.2 5.0 collective-permute-start.3
  67.5 5.4 collective-permute-start.7
  76.2 7.0 while.117
  83.3 24.4 %psum.120 = f32[2,512]{1,0:T(2,128)S(1)} all-reduce(f32[2,512]{1,0:T(2,128)S(1)} %dynamic_update_slice.40), channel_id=1, replica_groups=mesh['gx'=4,'gy'=8] {'gy'}, use_global_device_ids=true, to_apply=%region_4.0 | all-reduce | flops 1024 | bytes 8192 | tf_op jit(solution)/shard_map/psum | solution.py:144
  107.8 8.1 %psum.121 = f32[2,512]{1,0:T(2,128)S(1)} all-reduce(f32[2,512]{1,0:T(2,128)S(1)} %psum.120), channel_id=1, replica_groups=mesh['gx'=4,'gy'=8] {'gx'}, use_global_device_ids=true, to_apply=%region_5.0 | all-reduce | flops 1024 | bytes 8192 | tf_op jit(solution)/shard_map/psum | solution.py:144
  135.5 41.8 %all-reduce.29 = (f32[2,1]{0,1:T(1,128)S(1)}, f32[]{:T(128)}) all-reduce(f32[2,1]{0,1:T(1,128)S(1)} %maximum_bitcast_fusion.1, f32[]{:T(128)} %multiply_reduce_fusion.2), channel_id=1, replica_groups=mesh['gx'=4,'gy'=8] {'gx','gy'}, use_global_device_ids=true, to_apply=%region_10.0 | all-reduce | flops 3 | bytes 24 | tf_op jit(solution)/shard_map/psum | solution.py:181
  188.2 5.0 collective-permute-start.15
  204.0 5.6 collective-permute-start.19
  214.2 6.9 while.118
  221.3 24.6 %psum.124 = f32[2,512]{1,0:T(2,128)S(1)} all-reduce(f32[2,512]{1,0:T(2,128)S(1)} %dynamic_update_slice.41), channel_id=1, replica_groups=mesh['gx'=4,'gy'=8] {'gy'}, use_global_device_ids=true, to_apply=%region_16.0 | all-reduce | flops 1024 | bytes 8192 | tf_op jit(solution)/shard_map/psum | solution.py:144
  245.9 7.9 %psum.125 = f32[2,512]{1,0:T(2,128)S(1)} all-reduce(f32[2,512]{1,0:T(2,128)S(1)} %psum.124), channel_id=1, replica_groups=mesh['gx'=4,'gy'=8] {'gx'}, use_global_device_ids=true, to_apply=%region_17.0 | all-reduce | flops 1024 | bytes 8192 | tf_op jit(solution)/shard_map/psum | solution.py:144
  275.3 41.9 %all-reduce.28 = (f32[2,2]{0,1:T(2,128)S(1)}, f32[]{:T(128)}) all-reduce(f32[2,2]{0,1:T(2,128)S(1)} %pad_maximum_fusion.166, f32[]{:T(128)} %multiply_reduce_fusion.1), channel_id=1, replica_groups=mesh['gx'=4,'gy'=8] {'gx','gy'}, use_global_device_ids=true, to_apply=%region_24.0 | all-reduce | flops 5 | bytes 40 | tf_op jit(solution)/shard_map/psum | solution.py:181
  344.3 5.2 collective-permute-start.31
  355.0 6.9 while.119
  362.2 24.6 %psum.128 = f32[2,512]{1,0:T(2,128)S(1)} all-reduce(f32[2,512]{1,0:T(2,128)S(1)} %dynamic_update_slice.42), channel_id=1, replica_groups=mesh['gx'=4,'gy'=8] {'gy'}, use_global_device_ids=true, to_apply=%region_30.0 | all-reduce | flops 1024 | bytes 8192 | tf_op jit(solution)/shard_map/psum | solution.py:144
  386.7 8.1 %psum.129 = f32[2,512]{1,0:T(2,128)S(1)} all-reduce(f32[2,512]{1,0:T(2,128)S(1)} %psum.128), channel_id=1, replica_groups=mesh['gx'=4,'gy'=8] {'gx'}, use_global_device_ids=true, to_apply=%region_31.0 | all-reduce | flops 1024 | bytes 8192 | tf_op jit(solution)/shard_map/psum | solution.py:144
  418.9 41.9 %all-reduce.27 = (f32[2,3]{0,1:T(4,128)S(1)}, f32[]{:T(128)}) all-reduce(f32[2,3]{0,1:T(4,128)S(1)} %pad_maximum_fusion.161, f32[]{:T(128)} %multiply_reduce_fusion), channel_id=1, replica_groups=mesh['gx'=4,'gy'=8] {'gx','gy'}, use_global_device_ids=true, to_apply=%region_40.0 | all-reduce | flops 7 | bytes 56 | tf_op jit(solution)/shard_map/psum | solution.py:181
  477.9 5.1 collective-permute-start.39
  492.8 5.2 collective-permute-start.43
  502.7 6.9 while.120
  509.8 24.7 %psum.132 = f32[2,512]{1,0:T(2,128)S(1)} all-reduce(f32[2,512]{1,0:T(2,128)S(1)} %dynamic_update_slice.43), channel_id=1, replica_groups=mesh['gx'=4,'gy'=8] {'gy'}, use_global_device_ids=true, to_apply=%region_46.0 | all-reduce | flops 1024 | bytes 8192 | tf_op jit(solution)/shard_map/psum | solution.py:144
  534.5 7.3 psum.133
  570.9 42.1 %all-reduce.26 = (f32[2,4]{0,1:T(4,128)S(1)}, f32[]{:T(128)}) all-reduce(f32[2,4]{0,1:T(4,128)S(1)} %pad_maximum_fusion.162, f32[]{:T(128)} %fusion.133), channel_id=1, replica_groups=mesh['gx'=4,'gy'=8] {'gx','gy'}, use_global_device_ids=true, to_apply=%region_58.0 | all-reduce | flops 9 | bytes 72 | tf_op jit(solution)/shard_map/psum | solution.py:181
  (518 shorter events, 321.3 us)
Async XLA Ops:
  51.9 6.5 collective-permute-start.2
  53.2 6.5 collective-permute-start.3
  66.2 7.0 collective-permute-start.6
  67.5 6.9 collective-permute-start.7
  124.9 6.1 collective-permute-start.10
  126.2 6.0 collective-permute-start.11
  186.9 6.5 collective-permute-start.14
  188.2 6.4 collective-permute-start.15
  202.7 7.1 collective-permute-start.18
  204.0 6.6 collective-permute-start.19
  263.1 6.1 collective-permute-start.22
  264.4 6.0 collective-permute-start.23
  328.0 6.5 collective-permute-start.26
  329.3 6.4 collective-permute-start.27
  343.0 6.7 collective-permute-start.30
  344.3 6.6 collective-permute-start.31
  404.1 6.1 collective-permute-start.34
  405.4 6.0 collective-permute-start.35
  476.6 6.6 collective-permute-start.38
  477.9 6.5 collective-permute-start.39
  491.5 6.7 collective-permute-start.42
  492.8 6.6 collective-permute-start.43
  554.4 6.1 collective-permute-start.46
  555.7 6.0 collective-permute-start.47
  (92 other events, 973.7 us)
